TPU v7x, 128 devices: a whole 4x4x4 slice. The times are simulated.
128 devices in a mesh: row: 2 (over z_lo), col: 64 (over y, x, z_hi, core).
Axes of the slice: x: 4, y: 4, z: 4 (z_hi: 2, z_lo: 2; z = z_hi * 2 + z_lo), core: 2. Of those that a mesh axis runs over, the one named last changes fastest.
Arguments:
- tokens: bfloat16 [512, 4608], P('col', 'row'), may hold values from -6 to 6
- pre_gain: float32 [2, 4608], P(None, 'row'), may hold values from -0.6 to 0.6
- post_gain: float32 [2, 4608], P(None, 'row'), may hold values from -0.6 to 0.6
- gate_weight: bfloat16 [2, 4608, 36864], P(None, ('row', 'col')), may hold values from -0.09375 to 0.09375
- up_weight: bfloat16 [2, 4608, 36864], P(None, ('row', 'col')), may hold values from -0.09375 to 0.09375
- down_weight: bfloat16 [2, 36864, 4608], P(None, ('row', 'col')), may hold values from -0.13541667 to 0.13541667
Outputs:
- stream: bfloat16 [512, 4608], P('col', 'row')
All inputs are finite; a program needn't handle non-finite values.
Results may differ from a plain program's by a relative error of at most 0.019.
Values may be sent and summed in bfloat16 or wider, within the bound.
A program may use at most 128 MiB of HBM per device.

v0:
```python
import jax
import jax.numpy as jnp
from jax import lax
from jax.sharding import Mesh
from jax.sharding import PartitionSpec as P

COL = ("col_0", "col_1", "col_2", "col_3")
ROW_COL = ("row", "col_0", "col_1", "col_2", "col_3")


norm_eps = 1e-06


def sent_to_all(value, axis):
    copies = jnp.broadcast_to(value, (lax.axis_size(axis), *value.shape))
    return lax.all_to_all(copies, axis, split_axis=0, concat_axis=0, tiled=True)


def over_copies(value, axis):
    everything = sent_to_all(value, axis)
    return jnp.sum(everything, axis=0)


def laid_out(blocks, dim):
    lengths = list(blocks.shape[1:])
    lengths[dim] *= blocks.shape[0]
    return jnp.moveaxis(blocks, 0, dim).reshape(lengths)


def whole_of(value, axes, dim):
    far, near = axes
    first = sent_to_all(value, far)
    blocks = jnp.swapaxes(sent_to_all(first, near), 0, 1)
    return laid_out(blocks.reshape(-1, *value.shape), dim)


def over_copies_2(value, axis):
    everything = sent_to_all(value, axis)
    return jnp.sum(everything.astype(jnp.float32), axis=0)


def split_up(value, dim, peers):
    before, after = (value.shape[:dim], value.shape[dim + 1 :])
    return jnp.moveaxis(value.reshape(*before, peers, -1, *after), dim, 0)


def summed_on_arrival(value, axis, dim):
    peers = lax.axis_size(axis)
    blocks = lax.all_to_all(split_up(value, dim, peers), axis, 0, 0, tiled=True)
    return jnp.sum(blocks.astype(jnp.float32), axis=0)


def sum_by_axis(value, axes, dim):
    far, near = axes
    blocks = split_up(value, dim, lax.axis_size(far))
    nearer = summed_on_arrival(blocks, near, dim + 1)
    arrived = lax.all_to_all(
        nearer.astype(jnp.bfloat16), far, split_axis=0, concat_axis=0, tiled=True
    )
    return arrived.astype(jnp.float32).sum(axis=0)


def activate(summed, columns):
    gate = summed[:, :columns]
    up_proj = summed[:, columns:]
    return (jax.nn.gelu(gate, approximate=True) * up_proj).astype(jnp.bfloat16)


def on_device(tokens, pre_gain, post_gain, gate_weight, up_weight, down_weight):
    layer_count = gate_weight.shape[0]
    row_count = lax.axis_size("row")
    col_count = lax.axis_size(COL)
    model_width = tokens.shape[1] * row_count
    stored_rows = gate_weight.shape[1]
    hidden_total = gate_weight.shape[2]
    block_width = hidden_total // (row_count * col_count)
    tile_rows = stored_rows * col_count
    tile_columns = hidden_total // col_count
    gate_split = gate_weight.reshape(layer_count, stored_rows, row_count, col_count, block_width)
    up_split = up_weight.reshape(layer_count, stored_rows, row_count, col_count, block_width)
    gate_tiles, up_tiles = (
        lax.all_to_all(gate_split, COL, split_axis=3, concat_axis=1, tiled=True),
        lax.all_to_all(up_split, COL, split_axis=3, concat_axis=1, tiled=True),
    )
    gate_tiles = gate_tiles.reshape(layer_count, tile_rows, tile_columns)
    up_tiles = up_tiles.reshape(layer_count, tile_rows, tile_columns)
    down_tiles = lax.all_to_all(down_weight, "row", split_axis=2, concat_axis=1, tiled=True)
    current = tokens
    for layer_index in range(layer_count):
        gate_up = jnp.concatenate((gate_tiles[layer_index], up_tiles[layer_index]), axis=1)
        down_tile = down_tiles[layer_index]
        columns = gate_up.shape[1] // 2
        values = current.astype(jnp.float32)
        squares = over_copies(jnp.sum(values * values, axis=1), "row")
        scale_pre = lax.rsqrt(squares / model_width + norm_eps)[:, None]
        normed = (values * scale_pre * (1.0 + pre_gain[layer_index])[None, :]).astype(jnp.bfloat16)
        partial_sums = jnp.dot(
            whole_of(normed, (("col_0", "col_1", "col_2"), "col_3"), 0),
            gate_up,
            preferred_element_type=jnp.float32,
        )
        summed = over_copies_2(partial_sums.astype(jnp.bfloat16), "row").astype(jnp.float32)
        hidden = activate(summed, columns)
        branch = sum_by_axis(
            jnp.dot(hidden, down_tile, preferred_element_type=jnp.float32).astype(jnp.bfloat16),
            (("col_0", "col_1", "col_2"), "col_3"),
            0,
        )
        branch_squares = over_copies(jnp.sum(branch * branch, axis=1), "row")
        scale_post = lax.rsqrt(branch_squares / model_width + norm_eps)[:, None]
        post = branch * scale_post * (1.0 + post_gain[layer_index])[None, :]
        current = (values + post).astype(jnp.bfloat16)
    return current


def solution(mesh):
    split = Mesh(
        mesh.devices.reshape(mesh.shape["row"], 4, 4, 2, 2),
        ("row", "col_0", "col_1", "col_2", "col_3"),
    )
    in_specs = (
        P(COL, "row"),
        P(None, "row"),
        P(None, "row"),
        P(None, ROW_COL, None),
        P(None, ROW_COL, None),
        P(None, ROW_COL, None),
    )
    out_specs = P(COL, "row")
    return jax.shard_map(
        on_device, mesh=split, in_specs=in_specs, out_specs=out_specs, check_vma=False
    )
```

profile of v0, /device:TPU:0, one launch (start us, length us, event | category | flops | bytes accessed | tf_op | source)
XLA Modules:
  0.0 577.0 jit_solution(1357578688195838266)
XLA Ops:
  0.0 0.9 fusion.42
  1.5 3.3 all-to-all-start
  4.8 1.4 add_reduce_fusion.1
  6.2 2.3 all-to-all-done
  8.5 0.8 fusion.44
  9.3 1.1 broadcast_in_dim.39
  10.5 10.6 %all-to-all-start.1 = ((bf16[32,8,2304]{2,1,0:T(8,128)(2,1)}), bf16[32,8,2304]{2,1,0:T(8,128)(2,1)S(1)}, u32[]{:S(2)}, u32[]{:S(2)}) async-start(bf16[32,8,2304]{2,1,0:T(8,128)(2,1)} %broadcast_in_dim.39), calls=%async_computation.1 | async-start | bytes 2359296 | tf_op jit(solution)/shard_map/all_to_all | solution.py:16
  21.1 14.4 %reshape.58 = bf16[2,36,2,64,288]{4,3,2,0,1:T(8,128)(2,1)} reshape(bf16[2,36,36864]{2,0,1:T(2,128)(2,1)} %param.9) | data formatting | bytes 10616832 | tf_op jit(solution)/shard_map/reshape | solution.py:79
  35.5 11.5 %copy.43 = bf16[2,36,2,64,288]{4,2,1,0,3:T(2,128)(2,1)} copy(bf16[2,36,2,64,288]{4,3,2,0,1:T(8,128)(2,1)} %reshape.58) | data formatting | bytes 10616832 | tf_op jit(solution)/shard_map/reshape | solution.py:79
  47.1 5.6 all_to_all.119
  52.7 10.6 %all-to-all-start.3 = ((bf16[2,36,2,64,288]{4,2,1,0,3:T(2,128)(2,1)}), bf16[2,36,2,64,288]{4,2,1,0,3:T(2,128)(2,1)}, u32[]{:S(2)}, u32[]{:S(2)}) async-start(bf16[2,36,2,64,288]{4,2,1,0,3:T(2,128)(2,1)} %copy.43), calls=%async_computation.3 | async-start | bytes 14155776 | tf_op jit(solution)/shard_map/all_to_all | solution.py:82
  63.4 14.4 %reshape.59 = bf16[2,36,2,64,288]{4,3,2,0,1:T(8,128)(2,1)} reshape(bf16[2,36,36864]{2,0,1:T(2,128)(2,1)} %param.10) | data formatting | bytes 10616832 | tf_op jit(solution)/shard_map/reshape | solution.py:80
  77.8 11.5 %copy.44 = bf16[2,36,2,64,288]{4,2,1,0,3:T(2,128)(2,1)} copy(bf16[2,36,2,64,288]{4,3,2,0,1:T(8,128)(2,1)} %reshape.59) | data formatting | bytes 10616832 | tf_op jit(solution)/shard_map/reshape | solution.py:80
  89.3 62.8 %all-to-all-done.3 = bf16[2,36,2,64,288]{4,2,1,0,3:T(2,128)(2,1)} async-done(((bf16[2,36,2,64,288]{4,2,1,0,3:T(2,128)(2,1)}), bf16[2,36,2,64,288]{4,2,1,0,3:T(2,128)(2,1)}, u32[]{:S(2)}, u32[]{:S(2)}) %all-to-all-start.3) | async-done | bytes 5308448 | tf_op jit(solution)/shard_map/all_to_all | solution.py:82
  152.1 16.1 %all-to-all-start.4 = ((bf16[2,36,2,64,288]{4,2,1,0,3:T(2,128)(2,1)}), bf16[2,36,2,64,288]{4,2,1,0,3:T(2,128)(2,1)}, u32[]{:S(2)}, u32[]{:S(2)}) async-start(bf16[2,36,2,64,288]{4,2,1,0,3:T(2,128)(2,1)} %copy.44), calls=%async_computation.4 | async-start | bytes 14155776 | tf_op jit(solution)/shard_map/all_to_all | solution.py:83
  168.1 18.0 %copy.45 = bf16[2,288,4608]{1,0,2:T(2,128)(2,1)} copy(bf16[2,288,4608]{2,1,0:T(8,128)(2,1)} %param.11) | data formatting | bytes 10616832 | tf_op args[5]
  186.1 1.6 copy.42
  187.7 69.1 %all-to-all-done.4 = bf16[2,36,2,64,288]{4,2,1,0,3:T(2,128)(2,1)} async-done(((bf16[2,36,2,64,288]{4,2,1,0,3:T(2,128)(2,1)}), bf16[2,36,2,64,288]{4,2,1,0,3:T(2,128)(2,1)}, u32[]{:S(2)}, u32[]{:S(2)}) %all-to-all-start.4) | async-done | bytes 5308448 | tf_op jit(solution)/shard_map/all_to_all | solution.py:83
  256.8 7.0 %all-to-all-start.6 = ((bf16[2,288,4608]{1,0,2:T(2,128)(2,1)}), bf16[2,288,4608]{1,0,2:T(2,128)(2,1)}, u32[]{:S(2)}, u32[]{:S(2)}) async-start(bf16[2,288,4608]{1,0,2:T(2,128)(2,1)} %copy.45), calls=%async_computation.6 | async-start | bytes 14155776 | tf_op jit(solution)/shard_map/all_to_all | solution.py:87
  263.9 9.8 %fusion.61 = (bf16[1,64,36,2,1,288]{5,3,2,0,1,4:T(2,128)(2,1)S(1)}, bf16[1,64,36,2,1,288]{5,3,2,0,1,4:T(2,128)(2,1)}) fusion(bf16[2,64,36,2,1,288]{5,3,2,0,1,4:T(2,128)(2,1)} %bitcast.4), kind=kLoop, calls=%fused_computation.80 | loop fusion | bytes 10616832 | tf_op jit(solution)/shard_map/slice | solution.py:90
  273.7 8.1 %squeeze.22 = bf16[2304,576]{1,0:T(8,128)(2,1)} reshape(bf16[1,64,36,2,1,288]{5,3,2,0,1,4:T(2,128)(2,1)} %get-tuple-element.12) | data formatting | bytes 5308416 | tf_op jit(solution)/shard_map/squeeze | solution.py:90
  281.8 10.8 %fusion.62 = (bf16[1,64,36,2,1,288]{5,3,2,0,1,4:T(2,128)(2,1)}, bf16[1,64,36,2,1,288]{5,3,2,0,1,4:T(2,128)(2,1)}) fusion(bf16[2,64,36,2,1,288]{5,3,2,0,1,4:T(2,128)(2,1)} %bitcast.6), kind=kLoop, calls=%fused_computation.81 | loop fusion | bytes 10616832 | tf_op jit(solution)/shard_map/slice | solution.py:90
  292.6 8.0 %squeeze.23 = bf16[2304,576]{1,0:T(8,128)(2,1)} reshape(bf16[1,64,36,2,1,288]{5,3,2,0,1,4:T(2,128)(2,1)} %get-tuple-element.14) | data formatting | bytes 5308416 | tf_op jit(solution)/shard_map/squeeze | solution.py:90
  300.6 7.7 %fusion.11 = bf16[512,1152]{1,0:T(8,128)(2,1)} fusion(bf16[512,2304]{1,0:T(8,128)(2,1)} %bitcast.49, bf16[2304,576]{1,0:T(8,128)(2,1)} %squeeze.23, bf16[2304,576]{1,0:T(8,128)(2,1)} %squeeze.22), kind=kOutput, calls=%fused_computation.13 | convolution fusion | flops 2729115648 | bytes 8847360 | tf_op jit(solution)/shard_map/dot_general | solution.py:97
  308.2 34.0 %all-to-all-done.6 = bf16[2,288,4608]{1,0,2:T(2,128)(2,1)} async-done(((bf16[2,288,4608]{1,0,2:T(2,128)(2,1)}), bf16[2,288,4608]{1,0,2:T(2,128)(2,1)}, u32[]{:S(2)}, u32[]{:S(2)}) %all-to-all-start.6) | async-done | bytes 5308448 | tf_op jit(solution)/shard_map/all_to_all | solution.py:87
  342.2 2.8 broadcast_in_dim.41
  345.0 4.9 all-to-all-start.5
  350.0 33.0 %copy.55 = bf16[2,288,2,2304]{3,2,1,0:T(2,128)(2,1)} copy(bf16[2,288,2,2304]{1,0,3,2:T(2,128)(2,1)} %bitcast.7) | data formatting | bytes 10616832 | tf_op jit(solution)/shard_map/all_to_all | solution.py:87
  383.0 7.0 %fusion.63 = (bf16[1,2,288,2304]{3,1,2,0:T(2,128)(2,1)}, bf16[1,2,288,2304]{3,1,2,0:T(2,128)(2,1)S(1)}) fusion(bf16[2,2,288,2304]{3,1,2,0:T(2,128)(2,1)} %bitcast.44), kind=kLoop, calls=%fused_computation.82 | loop fusion | bytes 10616832 | tf_op jit(solution)/shard_map/slice | solution.py:91
  390.1 1.8 copy.47
  391.9 2.5 convert_reduce_fusion.1
  394.4 2.3 convolution_convert_fusion.1
  396.9 6.5 %all_to_all.120 = bf16[2,32,8,2304]{3,2,1,0:T(8,128)(2,1)} all-to-all(bf16[2,32,8,2304]{3,2,1,0:T(8,128)(2,1)S(1)} %bitcast.45), channel_id=1, replica_groups=mesh['row'=2,'col_0'=4,'col_1'=4,'col_2'=2,'col_3'=2] {'col_3'}, dimensions={0} | all-to-all | bytes 4718592 | tf_op jit(solution)/shard_map/all_to_all | solution.py:49
  403.4 3.4 reduce_sum.135
  406.8 15.8 %all-to-all-start.8 = ((bf16[32,8,2304]{2,1,0:T(8,128)(2,1)}), bf16[32,8,2304]{2,1,0:T(8,128)(2,1)}, u32[]{:S(2)}, u32[]{:S(2)}) async-start(bf16[32,8,2304]{2,1,0:T(8,128)(2,1)} %reduce_sum.135), calls=%async_computation.8 | async-start | bytes 2359296 | tf_op jit(solution)/shard_map/all_to_all | solution.py:57
  422.7 1.5 add_reduce_fusion
  424.1 19.6 %all-to-all-done.8 = bf16[32,8,2304]{2,1,0:T(8,128)(2,1)} async-done(((bf16[32,8,2304]{2,1,0:T(8,128)(2,1)}), bf16[32,8,2304]{2,1,0:T(8,128)(2,1)}, u32[]{:S(2)}, u32[]{:S(2)}) %all-to-all-start.8) | async-done | bytes 1179680 | tf_op jit(solution)/shard_map/all_to_all | solution.py:57
  443.7 1.4 convert_reduce_fusion.3
  445.1 0.6 copy-done.4
  445.9 6.2 %all_to_all.121 = f32[2,1,8]{2,1,0:T(1,128)S(1)} all-to-all(f32[2,1,8]{2,1,0:T(1,128)S(1)} %broadcast_in_dim.42), channel_id=1, replica_groups=mesh['row'=2,'col_0'=4,'col_1'=4,'col_2'=2,'col_3'=2] {'row'}, dimensions={0} | all-to-all | bytes 128 | tf_op jit(solution)/shard_map/all_to_all | solution.py:16
  452.6 0.7 add_rsqrt_fusion.2
  453.3 1.7 fusion.46
  455.0 6.1 %all_to_all.122 = f32[2,1,8]{2,1,0:T(1,128)S(1)} all-to-all(f32[2,1,8]{2,1,0:T(1,128)S(1)} %broadcast_in_dim.43), channel_id=1, replica_groups=mesh['row'=2,'col_0'=4,'col_1'=4,'col_2'=2,'col_3'=2] {'row'}, dimensions={0} | all-to-all | bytes 128 | tf_op jit(solution)/shard_map/all_to_all | solution.py:16
  461.7 0.7 add_rsqrt_fusion.1
  462.4 0.9 fusion.48
  463.3 1.1 broadcast_in_dim.44
  464.3 4.7 all-to-all-start.11
  469.0 4.0 squeeze.25
  473.0 6.9 %squeeze.26 = bf16[2304,576]{1,0:T(8,128)(2,1)S(1)} reshape(bf16[1,64,36,2,1,288]{5,3,2,0,1,4:T(2,128)(2,1)} %get-tuple-element.13) | data formatting | bytes 5308416 | tf_op jit(solution)/shard_map/squeeze | solution.py:90
  480.0 6.5 %all-to-all-done.11 = bf16[32,8,2304]{2,1,0:T(8,128)(2,1)} async-done(((bf16[32,8,2304]{2,1,0:T(8,128)(2,1)}), bf16[32,8,2304]{2,1,0:T(8,128)(2,1)}, u32[]{:S(2)}, u32[]{:S(2)}) %all-to-all-start.11) | async-done | bytes 1179680 | tf_op jit(solution)/shard_map/all_to_all | solution.py:16
  486.5 1.4 broadcast_in_dim.45
  487.9 5.6 all_to_all.123
  493.7 1.7 copy-done.1
  495.4 3.2 fusion.8
  498.6 1.6 broadcast_in_dim.46
  500.3 5.4 all-to-all-start.13
  505.7 1.8 copy.52
  507.5 26.5 %all-to-all-done.13 = bf16[2,512,1152]{2,1,0:T(8,128)(2,1)} async-done(((bf16[2,512,1152]{2,1,0:T(8,128)(2,1)}), bf16[2,512,1152]{2,1,0:T(8,128)(2,1)}, u32[]{:S(2)}, u32[]{:S(2)}) %all-to-all-start.13) | async-done | bytes 2359328 | tf_op jit(solution)/shard_map/all_to_all | solution.py:16
  534.0 2.4 convert_reduce_fusion
  536.4 2.3 convolution_convert_fusion
  538.9 5.6 all_to_all.124
  545.1 24.5 %all_to_all.125 = bf16[32,8,2304]{2,1,0:T(8,128)(2,1)S(1)} all-to-all(bf16[32,8,2304]{2,1,0:T(8,128)(2,1)S(1)} %reduce_sum.142), channel_id=1, replica_groups=mesh['row'=2,'col_0'=4,'col_1'=4,'col_2'=2,'col_3'=2] {'col_0','col_1','..., dimensions={0} | all-to-all | bytes 2359296 | tf_op jit(solution)/shard_map/all_to_all | solution.py:57
  569.9 6.1 %all_to_all.126 = f32[2,1,8]{2,1,0:T(1,128)S(1)} all-to-all(f32[2,1,8]{2,1,0:T(1,128)S(1)} %broadcast_in_dim.47), channel_id=1, replica_groups=mesh['row'=2,'col_0'=4,'col_1'=4,'col_2'=2,'col_3'=2] {'row'}, dimensions={0} | all-to-all | bytes 128 | tf_op jit(solution)/shard_map/all_to_all | solution.py:16
  576.0 0.7 fusion.49
  (30 shorter events, 3.5 us)
Async XLA Ops:
  1.5 7.0 %all-to-all-start = ((f32[2,1,8]{2,1,0:T(1,128)}), f32[2,1,8]{2,1,0:T(1,128)S(1)}, u32[]{:S(2)}, u32[]{:S(2)}) async-start(f32[2,1,8]{2,1,0:T(1,128)} %broadcast_in_dim.38), calls=%async_computation | async-start | bytes 2048 | tf_op jit(solution)/shard_map/all_to_all | solution.py:16
  10.5 36.5 %all-to-all-start.1 = ((bf16[32,8,2304]{2,1,0:T(8,128)(2,1)}), bf16[32,8,2304]{2,1,0:T(8,128)(2,1)S(1)}, u32[]{:S(2)}, u32[]{:S(2)}) async-start(bf16[32,8,2304]{2,1,0:T(8,128)(2,1)} %broadcast_in_dim.39), calls=%async_computation.1 | async-start | bytes 2359296 | tf_op jit(solution)/shard_map/all_to_all | solution.py:16
  52.7 99.3 %all-to-all-start.3 = ((bf16[2,36,2,64,288]{4,2,1,0,3:T(2,128)(2,1)}), bf16[2,36,2,64,288]{4,2,1,0,3:T(2,128)(2,1)}, u32[]{:S(2)}, u32[]{:S(2)}) async-start(bf16[2,36,2,64,288]{4,2,1,0,3:T(2,128)(2,1)} %copy.43), calls=%async_computation.3 | async-start | bytes 14155776 | tf_op jit(solution)/shard_map/all_to_all | solution.py:82
  152.1 104.7 %all-to-all-start.4 = ((bf16[2,36,2,64,288]{4,2,1,0,3:T(2,128)(2,1)}), bf16[2,36,2,64,288]{4,2,1,0,3:T(2,128)(2,1)}, u32[]{:S(2)}, u32[]{:S(2)}) async-start(bf16[2,36,2,64,288]{4,2,1,0,3:T(2,128)(2,1)} %copy.44), calls=%async_computation.4 | async-start | bytes 14155776 | tf_op jit(solution)/shard_map/all_to_all | solution.py:83
  256.8 85.4 %all-to-all-start.6 = ((bf16[2,288,4608]{1,0,2:T(2,128)(2,1)}), bf16[2,288,4608]{1,0,2:T(2,128)(2,1)}, u32[]{:S(2)}, u32[]{:S(2)}) async-start(bf16[2,288,4608]{1,0,2:T(2,128)(2,1)} %copy.45), calls=%async_computation.6 | async-start | bytes 14155776 | tf_op jit(solution)/shard_map/all_to_all | solution.py:87
  345.0 46.8 %all-to-all-start.5 = ((bf16[2,512,1152]{2,1,0:T(8,128)(2,1)}), bf16[2,512,1152]{2,1,0:T(8,128)(2,1)}, u32[]{:S(2)}, u32[]{:S(2)}) async-start(bf16[2,512,1152]{2,1,0:T(8,128)(2,1)} %broadcast_in_dim.41), calls=%async_computation.5 | async-start | bytes 4718592 | tf_op jit(solution)/shard_map/all_to_all | solution.py:16
  391.9 2.5 copy-start.2
  406.8 36.9 %all-to-all-start.8 = ((bf16[32,8,2304]{2,1,0:T(8,128)(2,1)}), bf16[32,8,2304]{2,1,0:T(8,128)(2,1)}, u32[]{:S(2)}, u32[]{:S(2)}) async-start(bf16[32,8,2304]{2,1,0:T(8,128)(2,1)} %reduce_sum.135), calls=%async_computation.8 | async-start | bytes 2359296 | tf_op jit(solution)/shard_map/all_to_all | solution.py:57
  445.1 0.6 copy-start.4
  464.3 22.1 %all-to-all-start.11 = ((bf16[32,8,2304]{2,1,0:T(8,128)(2,1)}), bf16[32,8,2304]{2,1,0:T(8,128)(2,1)}, u32[]{:S(2)}, u32[]{:S(2)}) async-start(bf16[32,8,2304]{2,1,0:T(8,128)(2,1)} %broadcast_in_dim.44), calls=%async_computation.11 | async-start | bytes 2359296 | tf_op jit(solution)/shard_map/all_to_all | solution.py:16
  493.5 1.8 copy-start.1
  500.3 5.5 copy-start
  500.3 33.7 %all-to-all-start.13 = ((bf16[2,512,1152]{2,1,0:T(8,128)(2,1)}), bf16[2,512,1152]{2,1,0:T(8,128)(2,1)}, u32[]{:S(2)}, u32[]{:S(2)}) async-start(bf16[2,512,1152]{2,1,0:T(8,128)(2,1)} %broadcast_in_dim.46), calls=%async_computation.13 | async-start | bytes 4718592 | tf_op jit(solution)/shard_map/all_to_all | solution.py:16
  507.5 28.9 %copy-start.3 = (bf16[1,2,288,2304]{3,2,1,0:T(8,128)(2,1)S(1)}, bf16[1,2,288,2304]{3,2,1,0:T(8,128)(2,1)}, u32[]{:S(2)}) copy-start(bf16[1,2,288,2304]{3,2,1,0:T(8,128)(2,1)} %copy.52) | copy-start | bytes 7962628
  545.1 30.9 %copy-start.5 = (bf16[8,2304]{1,0:T(8,128)(2,1)S(1)}, bf16[8,2304]{1,0:T(8,128)(2,1)}, u32[]{:S(2)}) copy-start(bf16[8,2304]{1,0:T(8,128)(2,1)} %get-tuple-element.10) | copy-start | bytes 110596
where the time goes:
time: 587 us; the launch traced here: 577 us
  waiting for transfers between devices  221 us (38%)
  local copies, waits for them, and re-layouts  174 us (30%)
  starting transfers between devices  78.5 us (13%)
  blocking collectives  66.3 us (11%)
  other arithmetic  21.2 us (4%)
  matrix products  15.6 us (3%)
    all_to_all x1, waiting for transfers between devices, on_device(): lax.all_to_all(up_split, COL, split_axis=3, concat_axis=1, tiled=True)  69.1 us
    all_to_all x1, waiting for transfers between devices, on_device(): lax.all_to_all(gate_split, COL, split_axis=3, concat_axis=1, tiled=True)  62.8 us
    all_to_all x5, waiting for transfers between devices, sent_to_all(): return lax.all_to_all(copies, axis, split_axis=0, concat_axis=0, tiled=True)  35.2 us
    all_to_all x1, waiting for transfers between devices, on_device(): lax.all_to_all(down_weight, 'row', split_axis=2, concat_axis=1, tiled=True)  34 us
    all_to_all x1, local copies, waits for them, and re-layouts, on_device(): lax.all_to_all(down_weight, 'row', split_axis=2, concat_axis=1, tiled=True)  33 us
    all_to_all x5, blocking collectives, sent_to_all(): return lax.all_to_all(copies, axis, split_axis=0, concat_axis=0, tiled=True)  29.7 us
    all_to_all x5, starting transfers between devices, sent_to_all(): return lax.all_to_all(copies, axis, split_axis=0, concat_axis=0, tiled=True)  29 us
    reshape x2, local copies, waits for them, and re-layouts, on_device(): up_weight.reshape(layer_count, stored_rows, row_count, col_count, block_w...  25.9 us
  transfers between devices with their start and end apart: 9, of which 7 were waited for; matrix products, arithmetic and copies ran while one was open for 30% of the time, Pallas kernels for 0%

commit v1 on v0

v1 whole, which is shorter than its diff:
```python
import functools
import math

import jax
import jax.numpy as jnp
from jax import lax
from jax.experimental import pallas as pl
from jax.experimental.pallas import tpu as pltpu
from jax.sharding import PartitionSpec as P

MESH = pl.DeviceIdType.MESH
EPS = 1e-06
D, FF, LAYERS, TOKENS = 4608, 36864, 2, 512
HALF = D // 2
THIRD = HALF // 3
ROWS = 36
SOURCES = 64
WIDE, NARROW = 640, 512
GROUP = WIDE + NARROW
PARTS = 2
PART = SOURCES // PARTS
STORED = 288
SPARE = 64
ORDER = (("z", "x", "y"), ("x", "y", "z"), ("y", "z", "x"))
F32, BF16 = jnp.float32, jnp.bfloat16


def slab_shape(d, full):
    z = 1 if d == "z" or "z" not in full else 2
    y = 1 if d == "y" or "y" not in full else 4
    x = 1 if d == "x" or "x" not in full else 4
    return (z, y, x, z)


def kernel(
    tok, pre, post, gate, up, down, out,
    wbuf, dbuf, xbuf, rbuf, acc, xcat, tile, hid, nbuf, psend, precv, ssend, srecv, branch, cur,
    *rest,
):
    rs_in = [[rest[t * 3 + i] for i in range(3)] for t in range(3)]
    (w_send, w_recv, d_send, d_recv, a0_send, a0_recv, ag_send, ag_recv, rs_send, rs_recv,
     p_send, p_recv, s_send, s_recv) = rest[9:]
    r = lax.axis_index("row")
    c = lax.axis_index("col")
    y, x, zh, core = c // 16, (c // 4) % 4, (c // 2) % 2, c % 2
    own = {"y": y, "x": x, "z": r * 2 + zh}
    wide = (zh + x + y) % 2 == 0

    def device(ty, tx, tz, tcore):
        return (tz // 2, ty * 16 + tx * 4 + (tz % 2) * 2 + tcore)

    def remote(src, dst, send, recv, where):
        return pltpu.make_async_remote_copy(
            src_ref=src, dst_ref=dst, send_sem=send, recv_sem=recv, device_id=where, device_id_type=MESH
        )

    def weight_start(tz, ty, tx, k, layer):
        tzl, tzh = tz // 2, tz % 2
        group = tzl * 16 + ty * 4 + tx
        twide = (tzh + tx + ty) % 2 == 0
        where = device(ty, tx, tz, r)
        me = (k == 0) & (core == r)
        for is_wide, width in ((True, WIDE), (False, NARROW)):
            start = group * GROUP + tzh * (NARROW if is_wide else WIDE)
            for m, ref in enumerate((gate, up)):
                src = ref.at[layer, :, pl.ds(pl.multiple_of(start, 128), width)]
                dst = wbuf.at[layer, m, c, :, pl.ds(0, width)]
                right = twide if is_wide else jnp.logical_not(twide)

                @pl.when(right & me)
                def _():
                    pltpu.make_async_copy(src, dst, w_recv.at[layer, y // 2]).start()

                @pl.when(right & jnp.logical_not(me))
                def _():
                    remote(src, dst, w_send.at[0], w_recv.at[layer, y // 2], where).start()

    def weights_start(layer, lo, hi):
        def body(k, carry):
            dz, dx, dy = k % 4, (k // 4) % 4, k // 16
            weight_start((own["z"] + dz) % 4, (y + dy) % 4, (x + dx) % 4, k, layer)
            return carry

        lax.fori_loop(lo, hi, body, 0)

    def weights_wait(layer, part):
        for is_wide, width in ((True, WIDE), (False, NARROW)):
            ref = wbuf.at[layer, :, pl.ds(part * PART, PART), :, pl.ds(0, width)]

            @pl.when(wide if is_wide else jnp.logical_not(wide))
            def _():
                pltpu.make_async_copy(ref, ref, w_recv.at[layer, part]).wait()

    def weights_sent():
        mine = core == r
        for is_wide in (True, False):
            right = wide if is_wide else jnp.logical_not(wide)

            def take(n_wide, n_narrow):
                big = wbuf.at[:, :, pl.ds(0, n_wide), :, pl.ds(0, WIDE)]
                small = wbuf.at[:, :, pl.ds(0, n_narrow), :, pl.ds(0, NARROW)]
                pltpu.make_async_copy(big, big, w_send.at[0]).wait()
                pltpu.make_async_copy(small, small, w_send.at[0]).wait()

            @pl.when(right & mine)
            def _():
                take(31 if is_wide else 32, 32 if is_wide else 31)

        @pl.when(jnp.logical_not(mine))
        def _():
            big = wbuf.at[:, :, pl.ds(0, 32), :, pl.ds(0, WIDE)]
            small = wbuf.at[:, :, pl.ds(0, 32), :, pl.ds(0, NARROW)]
            pltpu.make_async_copy(big, big, w_send.at[0]).wait()
            pltpu.make_async_copy(small, small, w_send.at[0]).wait()

    partner = (r, c + 1 - 2 * core)

    def down_each(case):
        for h in range(2):
            for k in range(2):
                here = (zh == h) & (core == k)
                start = 0 if h == 0 else NARROW
                case(here & wide, 0, STORED, h * 576 + k * STORED - start)
                start = 0 if h == 0 else WIDE
                if h == k:
                    case(here & jnp.logical_not(wide), 0, STORED, h * 576 + k * STORED - start)
                else:
                    first = 0 if h == 0 else SPARE
                    case(
                        here & jnp.logical_not(wide), first, STORED - SPARE,
                        h * 576 + k * STORED + first - start,
                    )

    def down_start():
        for layer in range(LAYERS):
            def case(condition, first, rows, to):
                src = down.at[layer, pl.ds(first, rows)]
                dst = dbuf.at[layer, pl.ds(to, rows)]

                @pl.when(condition)
                def _():
                    pltpu.make_async_copy(src, dst, d_recv.at[layer]).start()
                    remote(src, dst, d_send.at[0], d_recv.at[layer], partner).start()

            down_each(case)
            for h in range(2):
                giver = (zh == h) & (core == 1 - h) & jnp.logical_not(wide)
                src = down.at[layer, pl.ds(STORED - SPARE if h == 0 else 0, SPARE)]
                dst = dbuf.at[layer, pl.ds(0 if h == 0 else 576, SPARE)]

                @pl.when(giver)
                def _():
                    for k in range(2):
                        remote(
                            src, dst, d_send.at[0], d_recv.at[layer], (r, y * 16 + x * 4 + (1 - h) * 2 + k)
                        ).start()

    def down_wait(layer):
        for is_wide, width in ((True, WIDE), (False, NARROW)):
            ref = dbuf.at[layer, pl.ds(0, width)]

            @pl.when(wide if is_wide else jnp.logical_not(wide))
            def _():
                pltpu.make_async_copy(ref, ref, d_recv.at[layer]).wait()

    def down_sent():
        full = wide | (zh == core)

        @pl.when(full)
        def _():
            ref = dbuf.at[:, pl.ds(0, STORED)]
            pltpu.make_async_copy(ref, ref, d_send.at[0]).wait()

        @pl.when(jnp.logical_not(full))
        def _():
            ref = dbuf.at[:, pl.ds(0, STORED + SPARE)]
            pltpu.make_async_copy(ref, ref, d_send.at[0]).wait()

    def slots(buf, layer, third, at):
        def pick(v, n):
            return pl.ds(0, n) if v is None else pl.ds(v, 1)

        z = at["z"]
        return buf.at[
            layer, third,
            pick(None if z is None else z // 2, 2),
            pick(at["y"], 4),
            pick(at["x"], 4),
            pick(None if z is None else z % 2, 2),
        ]

    def target(d, k):
        where = {**own, d: (own[d] + k) % 4}
        return where, device(where["y"], where["x"], where["z"], core)

    def gather_copy(layer, third, i, k, incoming):
        d = ORDER[third][i]
        at = {e: (None if e in ORDER[third][:i] else own[e]) for e in "xyz"}
        _, where = target(d, k)
        if incoming:
            at[d] = (own[d] + 4 - k) % 4
        ref = slots(xbuf, layer, third, at)
        return remote(ref, ref, ag_send.at[layer, third, i, k - 1], ag_recv.at[layer, third, i, k - 1], where)

    def scatter_copy(layer, third, i, k, incoming):
        order = ORDER[third][::-1]
        d = order[i]
        at = {e: (None if e in order[i + 1:] else own[e]) for e in "xyz"}
        there, where = target(d, k)
        at[d] = there[d]
        dst = rs_in[third][i].at[layer, k - 1]
        src = dst if incoming else slots(rbuf, layer, third, at)
        return remote(src, dst, rs_send.at[layer, third, i, k - 1], rs_recv.at[layer, third, i, k - 1], where)

    def scatter_add(layer, third, i):
        order = ORDER[third][::-1]
        free = order[i + 1:]
        sizes = [4 for _ in free]
        count = math.prod(sizes) if sizes else 1
        buf = rs_in[third][i]

        def body(n, carry):
            at, inner = dict(own), {"z": 0, "y": 0, "x": 0}
            for e in free:
                at[e] = n % 4
                inner[e] = n % 4
                n = n // 4
            total = rbuf[layer, third, at["z"] // 2, at["y"], at["x"], at["z"] % 2].astype(F32)
            for k in range(3):
                total += buf[layer, k, inner["z"] // 2, inner["y"], inner["x"], inner["z"] % 2].astype(F32)
            if i < 2:
                rbuf[layer, third, at["z"] // 2, at["y"], at["x"], at["z"] % 2] = total.astype(BF16)
            else:
                branch[:, third * THIRD:(third + 1) * THIRD] = total
            return carry

        if count == 1:
            body(0, 0)
        else:
            lax.fori_loop(0, count, body, 0)

    def pair_sum(value, n):
        part = jnp.sum(value * value, axis=1, keepdims=True)
        ssend[n] = jnp.broadcast_to(part, (8, 128))
        copy = remote(ssend.at[n], srecv.at[n], s_send.at[n], s_recv.at[n], (1 - r, c))
        copy.start()
        copy.wait()
        return part + srecv[n][:, 0:1]

    def norm_in(layer):
        values = cur[...]
        scale = lax.rsqrt(pair_sum(values, 2 * layer) / D + EPS)
        normed = values * scale * (1.0 + pre[layer:layer + 1, :])
        for t in range(3):
            nbuf[layer, t] = normed[:, t * THIRD:(t + 1) * THIRD].astype(BF16)

    def home_copy(layer):
        home = (core + r) % 2
        where = (home, y * 16 + x * 4 + zh * 2 + r)
        return nbuf.at[layer], xbuf.at[layer, :, home, y, x, zh], where

    def home_start(layer):
        src, dst, where = home_copy(layer)
        me = (core == 0) & (r == 0)

        @pl.when(me)
        def _():
            pltpu.make_async_copy(src, dst, a0_recv.at[layer]).start()

        @pl.when(jnp.logical_not(me))
        def _():
            remote(src, dst, a0_send.at[layer], a0_recv.at[layer], where).start()

    def home_wait(layer):
        ref = xbuf.at[layer, :, r, y, x, zh]
        pltpu.make_async_copy(ref, ref, a0_recv.at[layer]).wait()

    def home_sent(layer):
        @pl.when(jnp.logical_not((core == 0) & (r == 0)))
        def _():
            ref = nbuf.at[layer]
            pltpu.make_async_copy(ref, ref, a0_send.at[layer]).wait()

    def gather(layer, between):
        home_start(layer)
        between(0)
        home_wait(layer)
        for i in range(3):
            for t in range(3):
                for k in (1, 3, 2):
                    gather_copy(layer, t, i, k, False).start()
            between(i + 1)
            for t in range(3):
                for k in (1, 3, 2):
                    gather_copy(layer, t, i, k, True).wait_recv()

    def spread(layer):
        for t in range(3):
            def put(n, carry):
                piece = xbuf[layer, t, n // 4, n % 4]
                rows = piece.astype(F32).reshape(64, THIRD).astype(BF16)
                xcat[pl.ds(pl.multiple_of(n * 64, 64), 64), t * THIRD:(t + 1) * THIRD] = rows
                return carry

            lax.fori_loop(0, 8, put, 0)

    def project(layer):
        def pack(part, n, carry):
            for m in range(2):
                blocks = [wbuf[layer, m, part * PART + n * 4 + s].astype(F32) for s in range(4)]
                rows = pl.ds(pl.multiple_of(n * 4 * ROWS, 16), 4 * ROWS)
                tile[m, rows] = jnp.concatenate(blocks, axis=0).astype(BF16)
            return carry

        def multiply(part, n, carry):
            rows = pl.ds(pl.multiple_of(n * 128, 128), 128)
            lanes = slice(part * PART * ROWS, (part + 1) * PART * ROWS)
            for m in range(2):
                value = jnp.dot(xcat[rows, lanes], tile[m], preferred_element_type=F32)
                if part > 0:
                    value += acc[m, rows]
                acc[m, rows] = value
            return carry

        for part in range(PARTS):
            weights_wait(layer, part)
            lax.fori_loop(0, PART // 4, functools.partial(pack, part), 0)
            lax.fori_loop(0, 4, functools.partial(multiply, part), 0)

    def activate(layer):
        for m in range(2):
            psend[layer, m] = acc[m, 256:512].astype(BF16)
        copy = remote(psend.at[layer], precv.at[layer], p_send.at[layer], p_recv.at[layer], partner)
        copy.start()
        copy.wait()
        g = acc[0, 0:256] + precv[layer, 0].astype(F32)
        u = acc[1, 0:256] + precv[layer, 1].astype(F32)
        column = lax.broadcasted_iota(jnp.int32, (256, WIDE), 1)
        live = wide | (column < NARROW)
        hidden = jnp.where(live, jax.nn.gelu(g, approximate=True) * u, 0.0)
        hid[...] = hidden.astype(BF16)

    def project_down(layer):
        down_wait(layer)
        for t in range(3):
            for half in range(2):
                lanes = slice(half * HALF + t * THIRD, half * HALF + (t + 1) * THIRD)
                part = jnp.dot(hid[...], dbuf[layer, :, lanes], preferred_element_type=F32)
                rbuf[layer, t, half] = part.reshape(4, 4, 2, 8, THIRD).astype(BF16)
            for k in (1, 3, 2):
                scatter_copy(layer, t, 0, k, False).start()

    def scatter(layer):
        for i in range(3):
            for t in range(3):
                for k in (1, 3, 2):
                    scatter_copy(layer, t, i, k, True).wait_recv()
                scatter_add(layer, t, i)
                if i < 2:
                    for k in (1, 3, 2):
                        scatter_copy(layer, t, i + 1, k, False).start()

    def norm_out(layer):
        total = branch[...]
        scale = lax.rsqrt(pair_sum(total, 2 * layer + 1) / D + EPS)
        post_norm = total * scale * (1.0 + post[layer:layer + 1, :])
        result = (cur[...] + post_norm).astype(BF16)
        if layer == LAYERS - 1:
            out[...] = result
        else:
            cur[...] = result.astype(F32)

    @pl.when(jnp.logical_not(wide))
    def _():
        dbuf[:, NARROW:WIDE] = jnp.zeros((LAYERS, WIDE - NARROW, D), BF16)

    cur[...] = tok[...].astype(F32)
    norm_in(0)
    gather(0, lambda n: weights_start(0, n * 16, n * 16 + 16))
    down_start()
    weights_start(1, 0, 64)
    for layer in range(LAYERS):
        if layer > 0:
            norm_in(layer)
            gather(layer, lambda n: None)
        spread(layer)
        project(layer)
        activate(layer)
        project_down(layer)
        scatter(layer)
        norm_out(layer)

    weights_sent()
    down_sent()
    for layer in range(LAYERS):
        home_sent(layer)
        for t in range(3):
            for i in range(3):
                for k in (1, 2, 3):
                    gather_copy(layer, t, i, k, False).wait_send()
                    scatter_copy(layer, t, i, k, False).wait_send()


def on_device(tokens, pre_gain, post_gain, gate_weight, up_weight, down_weight):
    vmem = pl.BlockSpec(memory_space=pltpu.VMEM)
    hbm = pl.BlockSpec(memory_space=pl.ANY)
    dma = pltpu.SemaphoreType.DMA
    landing = []
    for t in range(3):
        order = ORDER[t][::-1]
        for i in range(3):
            landing.append(pltpu.VMEM((LAYERS, 3, *slab_shape(order[i], order[i + 1:]), 8, THIRD), BF16))
    return pl.pallas_call(
        kernel,
        out_shape=jax.ShapeDtypeStruct(tokens.shape, BF16),
        in_specs=[vmem, vmem, vmem, hbm, hbm, hbm],
        out_specs=vmem,
        scratch_shapes=[
            pltpu.VMEM((LAYERS, 2, SOURCES, ROWS, WIDE), BF16),
            pltpu.VMEM((LAYERS, WIDE, D), BF16),
            pltpu.VMEM((LAYERS, 3, 2, 4, 4, 2, 8, THIRD), BF16),
            pltpu.VMEM((LAYERS, 3, 2, 4, 4, 2, 8, THIRD), BF16),
            pltpu.VMEM((2, TOKENS, WIDE), F32),
            pltpu.VMEM((TOKENS, HALF), BF16),
            pltpu.VMEM((2, PART * ROWS, WIDE), BF16),
            pltpu.VMEM((256, WIDE), BF16),
            pltpu.VMEM((LAYERS, 3, 8, THIRD), BF16),
            pltpu.VMEM((LAYERS, 2, 256, WIDE), BF16),
            pltpu.VMEM((LAYERS, 2, 256, WIDE), BF16),
            pltpu.VMEM((2 * LAYERS, 8, 128), F32),
            pltpu.VMEM((2 * LAYERS, 8, 128), F32),
            pltpu.VMEM((8, HALF), F32),
            pltpu.VMEM((8, HALF), F32),
            *landing,
            dma((1,)), dma((LAYERS, PARTS)), dma((1,)), dma((LAYERS,)), dma((LAYERS,)), dma((LAYERS,)),
            dma((LAYERS, 3, 3, 3)), dma((LAYERS, 3, 3, 3)), dma((LAYERS, 3, 3, 3)), dma((LAYERS, 3, 3, 3)),
            dma((LAYERS,)), dma((LAYERS,)), dma((2 * LAYERS,)), dma((2 * LAYERS,)),
        ],
        compiler_params=pltpu.CompilerParams(has_side_effects=True, vmem_limit_bytes=67043328),
    )(tokens, pre_gain, post_gain, gate_weight, up_weight, down_weight)


def solution(mesh):
    weights = P(None, ("row", "col"), None)
    return jax.shard_map(
        on_device,
        mesh=mesh,
        in_specs=(P("col", "row"), P(None, "row"), P(None, "row"), weights, weights, weights),
        out_specs=P("col", "row"),
        check_vma=False,
    )
```

time: 587 us -> 326 us (0.56); the launches traced: 577 us -> 326 us
  Pallas kernels: 0 us -> 311 us
  waiting for transfers between devices: 221 us -> 0 us
  local copies, waits for them, and re-layouts: 174 us -> 15 us
  starting transfers between devices: 78.5 us -> 0 us
  blocking collectives: 66.3 us -> 0 us
  other arithmetic: 21.2 us -> 0 us
  matrix products: 15.6 us -> 0 us
    pallas_call x0 -> x1, Pallas kernels: none -> 311 us  [on_device(): pl.pallas_call(kernel, out_shape=jax.ShapeDtypeStruct(tokens.shape, BF16)...]
    all_to_all x9 -> x0, waiting for transfers between devices: 221 us -> none  [the longest x1 69.1 us: on_device(): lax.all_to_all(up_split, COL, split_axis=3, concat_axis=1, tiled=True)]
    all_to_all x9 -> x0, starting transfers between devices: 78.5 us -> none  [the longest x5 29 us: sent_to_all(): return lax.all_to_all(copies, axis, split_axis=0, concat_axis=0, tiled=True)]
    all_to_all x8 -> x0, blocking collectives: 66.3 us -> none  [the longest x5 29.7 us: sent_to_all(): return lax.all_to_all(copies, axis, split_axis=0, concat_axis=0, tiled=True)]
    reshape x4 -> x0, local copies, waits for them, and re-layouts: 51.7 us -> none  [the longest x2 25.9 us: on_device(): up_weight.reshape(layer_count, stored_rows, row_count, col_count, block_w...]
    all_to_all x3 -> x0, local copies, waits for them, and re-layouts: 34.8 us -> none  [the longest x1 33 us: on_device(): lax.all_to_all(down_weight, 'row', split_axis=2, concat_axis=1, tiled=True)]
    slice x5 -> x0, local copies, waits for them, and re-layouts: 31.2 us -> none  [the longest x1 10.8 us: on_device(): up_tiles[layer_index]]
    squeeze x4 -> x0, local copies, waits for them, and re-layouts: 27.1 us -> none  [the longest x2 14.9 us: on_device(): up_tiles[layer_index]]
  transfers between devices with their start and end apart: 9 -> 0, of which waited for: 7 -> 0; matrix products, arithmetic and copies ran while one was open for 30% -> 0% of each run, Pallas kernels for 0% -> 0%
where the time goes in v1:
time: 326 us
  Pallas kernels  311 us (95%)
  local copies, waits for them, and re-layouts  15 us (5%)
    pallas_call x1, Pallas kernels, on_device(): pl.pallas_call(kernel, out_shape=jax.ShapeDtypeStruct(tokens.shape, BF16)...  311 us
    unnamed x5, local copies, waits for them, and re-layouts  15 us

profile of v1, /device:TPU:0, one launch (start us, length us, event | category | flops | bytes accessed | tf_op | source)
XLA Modules:
  0.0 325.6 jit_solution(10924998252991515935)
XLA Ops:
  0.0 0.0 copy-start
  0.0 8.1 %copy.7.gate = bf16[2,36,36864]{2,1,0:T(8,128)(2,1)} copy(bf16[2,36,36864]{2,0,1:T(2,128)(2,1)} %param.9) | data formatting | bytes 10616832 | tf_op args[3]
  8.1 0.0 copy-done
  8.1 5.5 %copy.8.up = bf16[2,36,36864]{2,1,0:T(8,128)(2,1)} copy(bf16[2,36,36864]{2,0,1:T(2,128)(2,1)S(1)} %copy-done) | data formatting | bytes 10616832 | tf_op args[4]
  13.6 310.6 %shard_map.64 = bf16[8,2304]{1,0:T(8,128)(2,1)} custom-call(bf16[8,2304]{1,0:T(8,128)(2,1)} %tok.1, f32[2,2304]{1,0:T(2,128)} %pre.1, f32[2,2304]{1,0:T(2,128)} %post.1, bf16[2,36,36864]{2,1,0:T(8,128)(2,1)} %copy.7.gate, bf16[2,36,36864]{2,1,0:T(8,128)(2,1)} %copy.8.up, bf16[2,288,4608]{2,1,0:T(8,128)(2,1)} %down.1), custom_call_target="tpu_custom_call" | custom-call | tf_op jit(solution)/shard_map/pallas_call | solution.py:413
  324.2 1.4 copy.10
Async XLA Ops:
  0.0 8.1 %copy-start = (bf16[2,36,36864]{2,0,1:T(2,128)(2,1)S(1)}, bf16[2,36,36864]{2,0,1:T(2,128)(2,1)}, u32[]{:S(2)}) copy-start(bf16[2,36,36864]{2,0,1:T(2,128)(2,1)} %param.10) | copy-start | bytes 15925252
